TPU v7x, 16 devices: a whole 2x2x2 slice. The times are simulated.
16 devices in a mesh: dp: 2 (over z), ep: 8 (over y, x, core).
Axes of the slice: x: 2, y: 2, z: 2, core: 2. Of those that a mesh axis runs over, the one named last changes fastest.
Arguments:
- x_tok: bfloat16 [2048, 2048], P(('dp', 'ep')), parts along dimension 0
- topk_idx: int32 [2048, 6], P(('dp', 'ep')), parts along dimension 0
- topk_w: float32 [2048, 6], P(('dp', 'ep')), parts along dimension 0
- w_in: bfloat16 [64, 2048, 1408], P('ep')
- w_out: bfloat16 [64, 1408, 2048], P('ep')
- shared_in: bfloat16 [2048, 2816], replicated
- shared_out: bfloat16 [2816, 2048], replicated
Outputs:
- output: bfloat16 [2048, 2048], P(('dp', 'ep')), parts along dimension 0
There are 2 independent parts. A program takes and returns all parts, laid end to end along the dimension named above; an argument that names none is the same for every part.
All inputs are finite; a program needn't handle non-finite values.
Results may differ from a plain program's by a relative error of at most 0.001.
Values are sent between devices in bfloat16 or wider.
A program may use at most 1 GiB of HBM per device.

v0:
```python
import jax
import jax.numpy as jnp
from jax import lax
from jax.sharding import PartitionSpec as P

LOAD_MULT = 3


def slot_tables(topk_idx, topk_w, num_experts, slot_cap):
    tok_rows, top_k = topk_idx.shape
    expert_hot = (topk_idx[:, :, None] == jnp.arange(num_experts, dtype=jnp.int32)).astype(jnp.int32)
    running = jnp.cumsum(expert_hot.reshape(tok_rows * top_k, num_experts), axis=0)
    slot_pos = jnp.sum(running.reshape(tok_rows, top_k, num_experts) * expert_hot, axis=2) - 1
    slot_hot = (slot_pos[:, :, None] == jnp.arange(slot_cap, dtype=jnp.int32)).astype(jnp.bfloat16)
    gate_hot = expert_hot.astype(jnp.bfloat16) * topk_w.astype(jnp.bfloat16)[:, :, None]
    combine = jnp.einsum('tje,tjc->tec', gate_hot, slot_hot, preferred_element_type=jnp.float32).astype(jnp.bfloat16)
    dispatch = (combine != 0).astype(jnp.bfloat16)
    return combine, dispatch


def solution(mesh):
    group_size = mesh.shape['ep']

    def local_layer(x_loc, idx_loc, gate_loc, w_in, w_out, shared_in, shared_out):
        tok_rows, top_k = idx_loc.shape
        num_experts = w_in.shape[0] * group_size
        slot_cap = min(tok_rows, LOAD_MULT * tok_rows * top_k // num_experts)
        combine, dispatch = slot_tables(idx_loc, gate_loc, num_experts, slot_cap)
        send_rows = jnp.einsum('tec,tm->ecm', dispatch, x_loc, preferred_element_type=jnp.float32).astype(jnp.bfloat16)
        recv_rows = lax.all_to_all(send_rows, 'ep', 0, 1, tiled=True)
        hidden = jax.nn.gelu(jnp.einsum('erm,emf->erf', recv_rows, w_in, preferred_element_type=jnp.float32), approximate=True).astype(jnp.bfloat16)
        expert_out = jnp.einsum('erf,efm->erm', hidden, w_out, preferred_element_type=jnp.float32).astype(jnp.bfloat16)
        back_rows = lax.all_to_all(expert_out, 'ep', 1, 0, tiled=True)
        routed = jnp.einsum('tec,ecm->tm', combine, back_rows, preferred_element_type=jnp.float32)
        shared_hidden = jax.nn.gelu(jnp.dot(x_loc, shared_in, preferred_element_type=jnp.float32), approximate=True).astype(jnp.bfloat16)
        shared_val = jnp.dot(shared_hidden, shared_out, preferred_element_type=jnp.float32)
        return (routed + shared_val).astype(jnp.bfloat16)

    tok_spec = P(('dp', 'ep'), None)
    expert_spec = P('ep', None, None)
    whole_spec = P(None, None)
    return jax.shard_map(local_layer, mesh=mesh, in_specs=(tok_spec, tok_spec, tok_spec, expert_spec, expert_spec, whole_spec, whole_spec), out_specs=tok_spec, check_vma=False)
```

profile of v0, /device:TPU:0, one launch (start us, length us, event | category | flops | bytes accessed | tf_op | source)
XLA Modules:
  0.0 362.2 jit_solution(4078259003747576028)
XLA Ops:
  0.0 0.0 copy-start
  0.0 0.9 copy.49
  0.9 0.1 eq.53
  1.0 0.1 eq.49
  1.2 1.8 reduce-window.6
  3.0 0.3 slice_reduce_fusion
  3.3 0.1 fusion.49
  3.4 0.1 sub.7
  3.5 0.7 convert_element_type.36
  4.2 0.1 copy.50
  4.4 2.0 fusion.40
  6.4 1.4 copy.54
  7.8 0.0 copy-done
  7.8 5.0 %convolution_convert_fusion.1 = bf16[64,36,2048]{2,0,1:T(8,128)(2,1)} fusion(bf16[128,2048]{1,0:T(8,128)(2,1)S(1)} %copy-done, bf16[128,64,36]{0,1,2:T(8,128)(2,1)S(1)} %copy.54), kind=kOutput, calls=%fused_computation.15 | convolution fusion | flops 1212973056 | bytes 10551296 | tf_op jit(solution)/shard_map/tec,tm->ecm/dot_general | solution.py:29
  12.8 13.0 %copy.55 = bf16[64,36,2048]{2,1,0:T(8,128)(2,1)} copy(bf16[64,36,2048]{2,0,1:T(8,128)(2,1)} %convolution_convert_fusion.1) | data formatting | bytes 18874368 | tf_op jit(solution)/shard_map/convert_element_type | solution.py:29
  25.8 123.4 %all_to_all.36 = bf16[64,36,2048]{2,1,0:T(8,128)(2,1)} all-to-all(bf16[64,36,2048]{2,1,0:T(8,128)(2,1)} %copy.55), channel_id=1, replica_groups=mesh['dp'=2,'ep'=8] {'ep'}, dimensions={0} | all-to-all | bytes 18874368 | tf_op jit(solution)/shard_map/all_to_all | solution.py:30
  149.3 13.8 %copy.57 = bf16[8,8,36,2048]{3,0,2,1:T(8,128)(2,1)} copy(bf16[8,8,36,2048]{3,2,0,1:T(8,128)(2,1)} %bitcast.48) | data formatting | bytes 18874368 | tf_op jit(solution)/shard_map/all_to_all | solution.py:30
  163.1 44.8 %fusion.7 = bf16[8,288,1408]{2,1,0:T(8,128)(2,1)} fusion(bf16[8,2048,1408]{2,1,0:T(8,128)(2,1)} %param.10, bf16[8,288,2048]{2,0,1:T(8,128)(2,1)} %bitcast.49), kind=kOutput, calls=%fused_computation.8 | convolution fusion | flops 13316751360 | bytes 62062592 | tf_op jit(solution)/shard_map/erm,emf->erf/dot_general | solution.py:31
  207.9 25.2 %convolution_convert_fusion = bf16[8,288,2048]{2,1,0:T(8,128)(2,1)} fusion(bf16[8,288,1408]{2,1,0:T(8,128)(2,1)} %fusion.7, bf16[8,1408,2048]{2,1,0:T(8,128)(2,1)} %param.11), kind=kOutput, calls=%fused_computation.14 | convolution fusion | flops 13292273664 | bytes 62062592 | tf_op jit(solution)/shard_map/erf,efm->erm/dot_general | solution.py:32
  233.1 12.6 %copy.59 = bf16[8,288,2048]{2,0,1:T(8,128)(2,1)} copy(bf16[8,288,2048]{2,1,0:T(8,128)(2,1)} %convolution_convert_fusion) | data formatting | bytes 18874368 | tf_op jit(solution)/shard_map/convert_element_type | solution.py:32
  245.6 5.0 %all-to-all-start.1 = ((bf16[8,288,2048]{2,0,1:T(8,128)(2,1)}), bf16[8,288,2048]{2,0,1:T(8,128)(2,1)}, u32[]{:S(2)}, u32[]{:S(2)}) async-start(bf16[8,288,2048]{2,0,1:T(8,128)(2,1)} %copy.59), calls=%async_computation.1 | async-start | bytes 18874368 | tf_op jit(solution)/shard_map/all_to_all | solution.py:33
  250.7 11.1 %fusion.33 = f32[128,2048]{1,0:T(8,128)S(1)} fusion(bf16[2816,2048]{1,0:T(8,128)(2,1)} %param.13, bf16[128,2048]{1,0:T(8,128)(2,1)S(1)} %copy-done, bf16[2048,2816]{1,0:T(8,128)(2,1)} %param.12), kind=kOutput, calls=%fused_computation.29 | convolution fusion | flops 2956034048 | bytes 24641536 | tf_op jit(solution)/shard_map/dot_general | solution.py:36
  261.8 94.1 %all-to-all-done.1 = bf16[8,288,2048]{2,0,1:T(8,128)(2,1)} async-done(((bf16[8,288,2048]{2,0,1:T(8,128)(2,1)}), bf16[8,288,2048]{2,0,1:T(8,128)(2,1)}, u32[]{:S(2)}, u32[]{:S(2)}) %all-to-all-start.1) | async-done | bytes 9437216 | tf_op jit(solution)/shard_map/all_to_all | solution.py:33
  355.9 5.9 %fusion.21 = bf16[128,2048]{1,0:T(8,128)(2,1)} fusion(f32[128,2048]{1,0:T(8,128)S(1)} %fusion.33, bf16[8,8,36,2048]{3,1,2,0:T(8,128)(2,1)} %bitcast.7, bf16[128,64,36]{0,1,2:T(8,128)(2,1)S(1)} %copy.54), kind=kOutput, calls=%fused_computation.18 | convolution fusion | flops 1208483840 | bytes 11599872 | tf_op jit(solution)/shard_map/tec,ecm->tm/dot_general | solution.py:34
  (3 shorter events, 0.0 us)
Async XLA Ops:
  0.0 7.8 %copy-start = (bf16[128,2048]{1,0:T(8,128)(2,1)S(1)}, bf16[128,2048]{1,0:T(8,128)(2,1)}, u32[]{:S(2)}) copy-start(bf16[128,2048]{1,0:T(8,128)(2,1)} %param.7) | copy-start | bytes 1572868
  245.6 110.3 %all-to-all-start.1 = ((bf16[8,288,2048]{2,0,1:T(8,128)(2,1)}), bf16[8,288,2048]{2,0,1:T(8,128)(2,1)}, u32[]{:S(2)}, u32[]{:S(2)}) async-start(bf16[8,288,2048]{2,0,1:T(8,128)(2,1)} %copy.59), calls=%async_computation.1 | async-start | bytes 18874368 | tf_op jit(solution)/shard_map/all_to_all | solution.py:33
where the time goes:
time: 369 us; the launch traced here: 362 us
  blocking collectives  123 us (33%)
  matrix products  94.1 us (26%)
  waiting for transfers between devices  94.1 us (26%)
  local copies, waits for them, and re-layouts  42.4 us (11%)
  starting transfers between devices  5.03 us (1%)
    all_to_all x1, blocking collectives, local_layer(): recv_rows = lax.all_to_all(send_rows, 'ep', 0, 1, tiled=True)  123 us
    all_to_all x1, waiting for transfers between devices, local_layer(): back_rows = lax.all_to_all(expert_out, 'ep', 1, 0, tiled=True)  94.1 us
    dot_general x1, matrix products, local_layer(): jnp.einsum('erm,emf->erf', recv_rows, w_in, preferred_element_type=jnp.fl...  44.8 us
    dot_general x1, matrix products, local_layer(): jnp.einsum('erf,efm->erm', hidden, w_out, preferred_element_type=jnp.floa...  25.2 us
    all_to_all x1, local copies, waits for them, and re-layouts, local_layer(): recv_rows = lax.all_to_all(send_rows, 'ep', 0, 1, tiled=True)  13.8 us
    convert_element_type x1, local copies, waits for them, and re-layouts, local_layer(): jnp.einsum('tec,tm->ecm', dispatch, x_loc, preferred_element_type=jnp.flo...  13 us
    convert_element_type x1, local copies, waits for them, and re-layouts, local_layer(): jnp.einsum('erf,efm->erm', hidden, w_out, preferred_element_type=jnp.floa...  12.6 us
    dot_general x1, matrix products, local_layer(): jnp.dot(shared_hidden, shared_out, preferred_element_type=jnp.float32)  11.1 us
  transfers between devices with their start and end apart: 1, of which 1 were waited for; matrix products, arithmetic and copies ran while one was open for 3% of the time, Pallas kernels for 0%

commit v1 on v0

v1 whole, which is shorter than its diff:
```python
import functools

import jax
import jax.numpy as jnp
from jax import lax
from jax.experimental import pallas as pl
from jax.experimental.pallas import tpu as pltpu
from jax.sharding import PartitionSpec as P

LOAD_MULT = 3
MESH = pl.DeviceIdType.MESH
BF = jnp.bfloat16
F32 = jnp.float32
NB1 = 6
NB2 = 8
KH = 256
CB = 256
CH = CB // 2


def gelu(z):
    return 0.5 * z * (1.0 + jnp.tanh(0.7978845608028654 * (z + 0.044715 * (z * z * z))))


def dot(a, b):
    return jnp.dot(a, b, preferred_element_type=F32)


def kernel(top_k, slots, x_hbm, meta_ref, w_in, w_out, sh_in, sh_out, y_ref,
           xall, metaall, hacc, hid, ring1, ring2, xg, disp, comb, obuf, pbuf, r0, r1, r2, s1, s2, acc, zs, shid,
           ag_s, ag_r, mt_s, mt_r, x_sem, g1, g2, p0s, p0r, p1s, p1r, p2s, p2r):
    me = lax.axis_index('ep')
    n_exp, d_model, ff = w_in.shape
    tok = x_hbm.shape[0]
    nh = d_model // KH
    nk = nh // 2
    nb = d_model // CB
    n_sh = sh_in.shape[1] // ff
    core = me % 2
    chip = me // 2
    cx = chip % 2
    cy = chip // 2
    pa = chip * 2 + (1 - core)
    xchip = cy * 2 + (1 - cx)
    ychip = (1 - cy) * 2 + cx
    dchip = (1 - cy) * 2 + (1 - cx)
    xn = xchip * 2 + core
    yn = ychip * 2 + core
    dn = dchip * 2 + core
    n_chunk1 = n_sh * nk + nk * n_exp
    per_b = n_exp + n_sh
    n_chunk2 = nb * per_b
    pre1 = n_sh * nk

    def rcopy(src, dst, ss, rs, dev):
        return pltpu.make_async_remote_copy(src_ref=src, dst_ref=dst, send_sem=ss, recv_sem=rs,
                                            device_id={'ep': dev}, device_id_type=MESH)

    def sh1_copy(i):
        return pltpu.make_async_copy(sh_in.at[pl.ds((i % nk) * 2 * KH, 2 * KH), pl.ds(pl.multiple_of((i // nk) * ff, 128), ff)],
                                     ring1.at[i % NB1], g1.at[i % NB1])

    def ex1_copy(n):
        m = n - pre1
        return pltpu.make_async_copy(w_in.at[m % n_exp, pl.ds((m // n_exp) * 2 * KH, 2 * KH), :], ring1.at[n % NB1], g1.at[n % NB1])

    def next1(n):
        @pl.when(n < pre1)
        def _():
            sh1_copy(n).start()

        @pl.when(jnp.logical_and(n >= pre1, n < n_chunk1))
        def _():
            ex1_copy(n).start()

    def ex2_copy(n):
        return pltpu.make_async_copy(w_out.at[n % per_b, :, pl.ds(pl.multiple_of((n // per_b) * CB, CB), CB)], ring2.at[n % NB2], g2.at[n % NB2])

    def sh2_copy(n):
        return pltpu.make_async_copy(sh_out.at[pl.ds((n % per_b - n_exp) * ff, ff), pl.ds(pl.multiple_of((n // per_b) * CB, CB), CB)],
                                     ring2.at[n % NB2], g2.at[n % NB2])

    def next2(n):
        @pl.when(jnp.logical_and(n < n_chunk2, n % per_b < n_exp))
        def _():
            ex2_copy(n).start()

        @pl.when(jnp.logical_and(n < n_chunk2, n % per_b >= n_exp))
        def _():
            sh2_copy(n).start()

    xin = [pltpu.make_async_copy(x_hbm.at[:, pl.ds(j * KH, KH)], xall.at[j, me], x_sem.at[j]) for j in range(nh)]
    for cp in xin:
        cp.start()
    for i in range(NB1):
        sh1_copy(i).start()

    barrier = pltpu.get_barrier_semaphore()
    for k in range(1, 8):
        pl.semaphore_signal(barrier, inc=1, device_id={'ep': lax.rem(me + k, 8)}, device_id_type=MESH)
    pl.semaphore_wait(barrier, 7)

    def meta_copy(k):
        return rcopy(meta_ref, metaall.at[me], mt_s.at[k - 1], mt_r.at[me], lax.rem(me + k, 8))

    for k in range(1, 8):
        meta_copy(k).start()
    metaall[me] = meta_ref[...]

    sent = []

    def push(j, origin, dev, tag):
        cp = rcopy(xall.at[j, origin], xall.at[j, origin], ag_s.at[j, tag], ag_r.at[j, origin], dev)
        cp.start()
        sent.append(cp)

    def arrived(j, origin):
        rcopy(xall.at[j, origin], xall.at[j, origin], ag_s.at[j, 0], ag_r.at[j, origin], pa).wait_recv()

    def own(j):
        if j < nh:
            push(j, me, xn, 1)
            push(j, me, yn, 2)
            push(j, me, pa, 0)

    def svc(j):
        if j < nh:
            arrived(j, xn)
            if j % 2 == 0:
                push(j, xn, yn, 3)
            push(j, xn, pa, 4)
            arrived(j, yn)
            if j % 2 == 1:
                push(j, yn, xn, 3)
            push(j, yn, pa, 5)
        own(j + 3)
        if j >= 1:
            arrived(j - 1, dn)
            push(j - 1, dn, pa, 6)

    def partner_wait(j):
        for ch in range(4):
            arrived(j, ch * 2 + (1 - core))

    for j in range(nh):
        xin[j].wait()
    for j in range(3):
        own(j)

    zs[...] = jnp.zeros_like(zs)
    def sh_step(i, carry):
        sh1_copy(i).wait()
        kk = i % nk
        lhs = jnp.concatenate([xall[2 * kk, me], xall[2 * kk + 1, me]], axis=1)
        zs[i // nk] += dot(lhs, ring1[i % NB1])
        next1(i + NB1)
        return carry

    lax.fori_loop(0, pre1, sh_step, 0)
    for i in range(n_sh):
        shid[i] = gelu(zs[i]).astype(BF)
    for i in range(NB2):
        next2(jnp.int32(i))

    for k in range(1, 8):
        o = lax.rem(me + k, 8)
        rcopy(meta_ref, metaall.at[o], mt_s.at[k - 1], mt_r.at[o], o).wait_recv()
    t2 = 2 * tok
    upper = (lax.broadcasted_iota(jnp.int32, (t2, t2), 0) < lax.broadcasted_iota(jnp.int32, (t2, t2), 1)).astype(F32).astype(BF)
    expert_id = (lax.broadcasted_iota(jnp.int32, (n_exp, t2), 0) + me * n_exp).astype(F32)
    slot_id = lax.broadcasted_iota(jnp.int32, (slots, t2), 0).astype(F32)
    for q in range(4):
        mq = jnp.concatenate([metaall[2 * q], metaall[2 * q + 1]], axis=1)
        hot = jnp.zeros((n_exp, t2), F32)
        gate = jnp.zeros((n_exp, t2), F32)
        for j in range(top_k):
            eq = mq[j:j + 1, :] == expert_id
            hot += jnp.where(eq, 1.0, 0.0)
            gate += jnp.where(eq, mq[top_k + j:top_k + j + 1, :], 0.0)
        pos = dot(hot.astype(BF), upper)
        code = jnp.where(hot > 0.5, pos, -1.0)
        gated = []
        for e in range(n_exp):
            eq = slot_id == code[e:e + 1, :]
            disp[q, e * slots:(e + 1) * slots, :] = jnp.where(eq, 1.0, 0.0).astype(BF)
            gated.append(jnp.where(eq, gate[e:e + 1, :], 0.0))
        comb[q] = jnp.concatenate(gated, axis=0).T.astype(BF)

    def gather_rows(k):
        for q in range(4):
            for hf in range(2):
                xq = xall[2 * k + hf, 2 * q:2 * q + 2].reshape(t2, KH)
                rows = dot(disp[q], xq).astype(BF)
                for e in range(n_exp):
                    xg[e, q * slots:(q + 1) * slots, hf * KH:(hf + 1) * KH] = rows[e * slots:(e + 1) * slots, :]

    def ex_steps(k, lo, hi):
        def step(e, carry):
            n = pre1 + k * n_exp + e
            ex1_copy(n).wait()
            z = dot(xg[e], ring1[n % NB1])
            if k > 0:
                z += hacc[e]
            if k < nk - 1:
                hacc[e] = z
            else:
                hid[e] = gelu(z).astype(BF)
            next1(n + NB1)
            return carry
        lax.fori_loop(lo, hi, step, 0)

    svc(0)
    svc(1)
    svc(2)
    for k in range(nk):
        partner_wait(2 * k)
        partner_wait(2 * k + 1)
        gather_rows(k)
        ex_steps(k, 0, n_exp // 2)
        if 2 * k + 3 <= nh:
            svc(2 * k + 3)
        ex_steps(k, n_exp // 2, n_exp)
        if 2 * k + 4 <= nh:
            svc(2 * k + 4)

    def c0(b):
        return rcopy(pbuf.at[b % 2, 1 - core], r0.at[b], p0s.at[b], p0r.at[b], pa)

    def c1(b, h):
        return rcopy(s1.at[b, h], r1.at[b, h], p1s.at[b, h], p1r.at[b, h], (xn, yn)[h])

    def c2(b, h):
        return rcopy(s2.at[b, h], r2.at[b, h], p2s.at[b, h], p2r.at[b, h], (yn, xn)[h])

    def svc1(b):
        c0(b).wait_recv()
        slot = b % 2
        lo, hi = slice(0, CH), slice(CH, CB)

        def q_sum(q, cols):
            return pbuf[slot, core, q, :, cols] + r0[b, q, :, cols]

        for i in range(2):
            s1[b, 0, i] = q_sum(i * 2 + (1 - cx), lo)
            s1[b, 1, i] = q_sum((1 - cy) * 2 + i, hi)
        c1(b, 0).start()
        c1(b, 1).start()
        s2[b, 0] = q_sum(ychip, lo)
        s2[b, 1] = q_sum(xchip, hi)
        acc[b, :, lo] += q_sum(chip, lo)
        acc[b, :, hi] += q_sum(chip, hi)
        c0(b).wait_send()

    def svc2(b):
        c1(b, 0).wait_recv()
        s2[b, 0] += r1[b, 0, 1 - cy]
        c2(b, 0).start()
        c1(b, 1).wait_recv()
        s2[b, 1] += r1[b, 1, 1 - cx]
        c2(b, 1).start()
        acc[b, :, :CH] += r1[b, 0, cy]
        acc[b, :, CH:] += r1[b, 1, cx]

    def fin(b):
        c2(b, 0).wait_recv()
        c2(b, 1).wait_recv()
        cols = pl.multiple_of(b * CB, CB)
        y_ref[:, pl.ds(cols, CH)] = (acc[b, :, :CH] + r2[b, 0]).astype(BF)
        y_ref[:, pl.ds(pl.multiple_of(cols + CH, CH), CH)] = (acc[b, :, CH:] + r2[b, 1]).astype(BF)

    def block(b, carry):
        def step(e, c):
            n = b * per_b + e
            ex2_copy(n).wait()
            o = dot(hid[e], ring2[n % NB2]).astype(BF)
            for q in range(4):
                obuf[q, pl.ds(pl.multiple_of(e * slots, 16), slots), :] = o[q * slots:(q + 1) * slots, :]
            next2(n + NB2)
            return c
        lax.fori_loop(0, n_exp, step, 0)
        u = None
        for i in range(n_sh):
            n = b * per_b + n_exp + i
            sh2_copy(n).wait()
            v = dot(shid[i], ring2[n % NB2])
            u = v if u is None else u + v
            next2(n + NB2)
        acc[b] = u
        for q in range(4):
            part = dot(comb[q], obuf[q])
            pbuf[b % 2, 0, q] = part[:tok]
            pbuf[b % 2, 1, q] = part[tok:]
        c0(b).start()

        @pl.when(b >= 1)
        def _():
            svc1(b - 1)

        @pl.when(b >= 2)
        def _():
            svc2(b - 2)

        @pl.when(b >= 4)
        def _():
            fin(b - 4)
        return carry

    lax.fori_loop(0, nb, block, 0)
    svc1(nb - 1)
    svc2(nb - 2)
    fin(nb - 4)
    svc2(nb - 1)
    for b in range(nb - 3, nb):
        fin(b)

    for cp in sent:
        cp.wait_send()
    for k in range(1, 8):
        meta_copy(k).wait_send()
    for b in range(nb):
        for h in range(2):
            c1(b, h).wait_send()
            c2(b, h).wait_send()


def solution(mesh):
    group_size = mesh.shape['ep']

    def local_layer(x_loc, idx_loc, gate_loc, w_in, w_out, shared_in, shared_out):
        tok, top_k = idx_loc.shape
        n_exp, d_model, ff = w_in.shape
        n_sh = shared_in.shape[1] // ff
        cap = min(tok, LOAD_MULT * tok * top_k // (n_exp * group_size))
        slots = -(-2 * cap // 16) * 16
        rows = 4 * slots
        nh, nb = d_model // KH, d_model // CB
        meta = jnp.concatenate([idx_loc.astype(F32).T, gate_loc.T, jnp.zeros((16 - 2 * top_k, tok), F32)], axis=0)
        any_spec = pl.BlockSpec(memory_space=pl.ANY)
        vmem_spec = pl.BlockSpec(memory_space=pltpu.VMEM)
        dma = pltpu.SemaphoreType.DMA
        return pl.pallas_call(
            functools.partial(kernel, top_k, slots),
            out_shape=jax.ShapeDtypeStruct((tok, d_model), BF),
            in_specs=[any_spec, vmem_spec, any_spec, any_spec, any_spec, any_spec],
            out_specs=vmem_spec,
            scratch_shapes=[
                pltpu.VMEM((nh, group_size, tok, KH), BF),
                pltpu.VMEM((group_size, 16, tok), F32),
                pltpu.VMEM((n_exp, rows, ff), F32),
                pltpu.VMEM((n_exp, rows, ff), BF),
                pltpu.VMEM((NB1, 2 * KH, ff), BF),
                pltpu.VMEM((NB2, ff, CB), BF),
                pltpu.VMEM((n_exp, rows, 2 * KH), BF),
                pltpu.VMEM((4, n_exp * slots, 2 * tok), BF),
                pltpu.VMEM((4, 2 * tok, n_exp * slots), BF),
                pltpu.VMEM((4, n_exp * slots, CB), BF),
                pltpu.VMEM((2, 2, 4, tok, CB), F32),
                pltpu.VMEM((nb, 4, tok, CB), F32),
                pltpu.VMEM((nb, 2, 2, tok, CH), F32),
                pltpu.VMEM((nb, 2, tok, CH), F32),
                pltpu.VMEM((nb, 2, 2, tok, CH), F32),
                pltpu.VMEM((nb, 2, tok, CH), F32),
                pltpu.VMEM((nb, tok, CB), F32),
                pltpu.VMEM((n_sh, tok, ff), F32),
                pltpu.VMEM((n_sh, tok, ff), BF),
                dma((nh, 7)), dma((nh, 8)), dma((7,)), dma((8,)), dma((nh,)), dma((NB1,)), dma((NB2,)),
                dma((nb,)), dma((nb,)), dma((nb, 2)), dma((nb, 2)), dma((nb, 2)), dma((nb, 2)),
            ],
            compiler_params=pltpu.CompilerParams(collective_id=0, has_side_effects=True, vmem_limit_bytes=67043328),
        )(x_loc, meta, w_in, w_out, shared_in, shared_out)

    tok_spec = P(('dp', 'ep'), None)
    expert_spec = P('ep', None, None)
    whole_spec = P(None, None)
    return jax.shard_map(local_layer, mesh=mesh, in_specs=(tok_spec, tok_spec, tok_spec, expert_spec, expert_spec, whole_spec, whole_spec), out_specs=tok_spec, check_vma=False)
```

time: 369 us -> 104 us (0.28); the launches traced: 362 us -> 104 us
  blocking collectives: 123 us -> 0 us
  Pallas kernels: 0 us -> 100 us
  matrix products: 94.1 us -> 0 us
  waiting for transfers between devices: 94.1 us -> 0 us
  local copies, waits for them, and re-layouts: 42.4 us -> 1.96 us
  starting transfers between devices: 5.03 us -> 0 us
    all_to_all x1 -> x0, blocking collectives: 123 us -> none  [local_layer(): recv_rows = lax.all_to_all(send_rows, 'ep', 0, 1, tiled=True)]
    pallas_call x0 -> x1, Pallas kernels: none -> 100 us  [local_layer(): pl.pallas_call(functools.partial(kernel, top_k, slots), out_shape=jax.Sha...]
    dot_general x6 -> x0, matrix products: 94.1 us -> none  [the longest x1 44.8 us: local_layer(): jnp.einsum('erm,emf->erf', recv_rows, w_in, preferred_element_type=jnp.fl...]
    all_to_all x1 -> x0, waiting for transfers between devices: 94.1 us -> none  [local_layer(): back_rows = lax.all_to_all(expert_out, 'ep', 1, 0, tiled=True)]
    convert_element_type x3 -> x0, local copies, waits for them, and re-layouts: 25.7 us -> none  [the longest x1 13 us: local_layer(): jnp.einsum('tec,tm->ecm', dispatch, x_loc, preferred_element_type=jnp.flo...]
    all_to_all x1 -> x0, local copies, waits for them, and re-layouts: 13.8 us -> none  [local_layer(): recv_rows = lax.all_to_all(send_rows, 'ep', 0, 1, tiled=True)]
    all_to_all x1 -> x0, starting transfers between devices: 5.03 us -> none  [local_layer(): back_rows = lax.all_to_all(expert_out, 'ep', 1, 0, tiled=True)]
  transfers between devices with their start and end apart: 1 -> 0, of which waited for: 1 -> 0; matrix products, arithmetic and copies ran while one was open for 3% -> 0% of each run, Pallas kernels for 0% -> 0%
where the time goes in v1:
time: 104 us
  Pallas kernels  100 us (96%)
  other arithmetic  2.04 us (2%)
  local copies, waits for them, and re-layouts  1.96 us (2%)
    pallas_call x1, Pallas kernels, local_layer(): pl.pallas_call(functools.partial(kernel, top_k, slots), out_shape=jax.Sha...  100 us

profile of v1, /device:TPU:0, one launch (start us, length us, event | category | flops | bytes accessed | tf_op | source)
XLA Modules:
  0.0 104.1 jit_solution(213786414123042594)
XLA Ops:
  0.0 0.1 pad.2.clone
  0.1 0.7 convert_bitcast_fusion
  0.8 1.4 %maximum_maximum_fusion.meta_ref = f32[16,128]{1,0:T(8,128)} fusion(f32[6,128]{1,0:T(8,128)} %bitcast.3, f32[6,128]{1,0:T(8,128)S(1)} %convert_bitcast_fusion, f32[16]{0:T(128)S(1)} %pad.2.clone), kind=kLoop, calls=%fused_computation | loop fusion | flops 4096 | bytes 14400 | tf_op jit(solution)/shard_map/concatenate | solution.py:337
  2.1 100.1 %shard_map.73 = bf16[128,2048]{1,0:T(8,128)(2,1)} custom-call(bf16[128,2048]{1,0:T(8,128)(2,1)} %x_hbm.1, f32[16,128]{1,0:T(8,128)} %maximum_maximum_fusion.meta_ref, bf16[8,2048,1408]{2,1,0:T(8,128)(2,1)} %w_in.1, bf16[8,1408,2048]{2,1,0:T(8,128)(2,1)} %w_out.1, bf16[2048,2816]{1,0:T(8,128)(2,1)} %sh_in.1, bf16[2816,2048]{1,0:T(8,128)(2,1)} %sh_out.1), custom_call_target="tpu_custom_call" | custom-call | tf_op jit(solution)/shard_map/pallas_call | solution.py:341
  102.3 1.9 %copy.9 = bf16[128,2048]{1,0:T(8,128)(2,1)} copy(bf16[128,2048]{1,0:T(8,128)(2,1)} %shard_map.73) | data formatting | bytes 1048576
  (1 shorter events, 0.0 us)

commit v2 on v1

v2 whole, which is shorter than its diff:
```python
import functools

import jax
import jax.numpy as jnp
from jax import lax
from jax.experimental import pallas as pl
from jax.experimental.pallas import tpu as pltpu
from jax.sharding import PartitionSpec as P

LOAD_MULT = 3
MESH = pl.DeviceIdType.MESH
BF = jnp.bfloat16
F32 = jnp.float32
NB1 = 8
GRP = 2
KH = 256
CB = 256
CH = CB // 2


def gelu(z):
    half = 0.5 * z
    return half + half * jnp.tanh(z * (0.7978845608028654 + 0.03567740813636141 * (z * z)))


def dot(a, b):
    return jnp.dot(a, b, preferred_element_type=F32)


def kernel(top_k, slots, x_hbm, idx_ref, gate_ref, w_in, w_out, sh_in, sh_out, y_ref,
           xall, idxall, gateall, hacc, hid, ring1, ring2, xg, disp, comb, obuf, pbuf, r0, r1, r2, s1, s2, acc, shid,
           ag_s, ag_r, mi_s, mi_r, mg_s, mg_r, x_sem, g1, g2, p0s, p0r, p1s, p1r, p2s, p2r):
    me = lax.axis_index('ep')
    n_exp, d_model, ff = w_in.shape
    tok = x_hbm.shape[0]
    nh = d_model // KH
    nk = nh // 2
    nb = d_model // CB
    n_sh = sh_in.shape[1] // ff
    per = n_exp // n_sh
    core = me % 2
    chip = me // 2
    cx = chip % 2
    cy = chip // 2
    pa = chip * 2 + (1 - core)
    xchip = cy * 2 + (1 - cx)
    ychip = (1 - cy) * 2 + cx
    dchip = (1 - cy) * 2 + (1 - cx)
    xn = xchip * 2 + core
    yn = ychip * 2 + core
    dn = dchip * 2 + core
    pre1 = n_sh * nk
    n_chunk1 = pre1 + nk * n_exp

    def rcopy(src, dst, ss, rs, dev):
        return pltpu.make_async_remote_copy(src_ref=src, dst_ref=dst, send_sem=ss, recv_sem=rs,
                                            device_id={'ep': dev}, device_id_type=MESH)

    def copy1(n):
        slot = n % NB1
        if n < pre1:
            src = sh_in.at[pl.ds((n % nk) * 2 * KH, 2 * KH), pl.ds((n // nk) * ff, ff)]
        else:
            m = n - pre1
            src = w_in.at[m % n_exp, pl.ds((m // n_exp) * 2 * KH, 2 * KH), :]
        return pltpu.make_async_copy(src, ring1.at[slot], g1.at[slot])

    def start1(n):
        if n < n_chunk1:
            copy1(n).start()

    def copy2s(half, i):
        src = sh_out.at[pl.ds((i // per) * ff, ff), pl.ds((half * per + i % per) * CB, CB)]
        return pltpu.make_async_copy(src, ring2.at[half, i], g2.at[half, i])

    def copy2(b, e):
        src = w_out.at[e, :, pl.ds(pl.multiple_of(b * CB, CB), CB)]
        return pltpu.make_async_copy(src, ring2.at[b % 2, e], g2.at[b % 2, e])

    xin = [pltpu.make_async_copy(x_hbm.at[:, pl.ds(j * KH, KH)], xall.at[j, me], x_sem.at[j]) for j in range(nh)]
    for cp in xin:
        cp.start()
    for i in range(NB1):
        start1(i)

    barrier = pltpu.get_barrier_semaphore()
    for k in range(1, 8):
        pl.semaphore_signal(barrier, inc=1, device_id={'ep': lax.rem(me + k, 8)}, device_id_type=MESH)
    for half in range(2):
        for i in range(n_exp):
            copy2s(half, i).start()
    for cp in xin:
        cp.wait()
    pl.semaphore_wait(barrier, 7)

    sent = []

    def push(j, origin, dev, tag):
        cp = rcopy(xall.at[j, origin], xall.at[j, origin], ag_s.at[j, tag], ag_r.at[j, origin], dev)
        cp.start()
        sent.append(cp)

    def arrived(j, origin):
        rcopy(xall.at[j, origin], xall.at[j, origin], ag_s.at[j, 0], ag_r.at[j, origin], pa).wait_recv()

    def own(j):
        push(j, me, xn, 1)
        push(j, me, yn, 2)
        push(j, me, dn, 3)
        push(j, me, pa, 0)

    def svc_a(j):
        if j < nh:
            arrived(j, xn)
            push(j, xn, pa, 4)
            arrived(j, yn)
            push(j, yn, pa, 5)

    def svc_d(j):
        if j < nh:
            arrived(j, dn)
            push(j, dn, pa, 6)

    def partner_wait(j):
        for ch in range(4):
            arrived(j, ch * 2 + (1 - core))

    own(0)

    def meta_copies(k, o):
        dev = lax.rem(me + k, 8)
        return (rcopy(idx_ref, idxall.at[o], mi_s.at[k - 1], mi_r.at[o], dev),
                rcopy(gate_ref, gateall.at[o], mg_s.at[k - 1], mg_r.at[o], dev))

    for k in range(1, 8):
        for cp in meta_copies(k, me):
            cp.start()
    idxall[me] = idx_ref[...]
    gateall[me] = gate_ref[...]
    for j in range(1, nh):
        own(j)

    xk = [jnp.concatenate([xall[2 * k, me], xall[2 * k + 1, me]], axis=1) for k in range(nk)]
    for i in range(n_sh):
        z = None
        for k in range(nk):
            copy1(i * nk + k).wait()
        for k in range(nk):
            v = dot(xk[k], ring1[(i * nk + k) % NB1])
            z = v if z is None else z + v
        shid[i] = gelu(z).astype(BF)
        for k in range(nk):
            start1(i * nk + k + NB1)

    def sh_out_half(half):
        for i in range(n_exp):
            copy2s(half, i).wait()
        for i in range(per):
            acc[half * per + i] = sum(dot(shid[m], ring2[half, m * per + i]) for m in range(n_sh))
        for e in range(n_exp):
            copy2(half, e).start()

    svc_a(0)
    svc_d(0)

    for k in range(1, 8):
        for cp in meta_copies(k, lax.rem(me + k, 8)):
            cp.wait_recv()
    t2 = 2 * tok
    upper = (lax.broadcasted_iota(jnp.int32, (t2, t2), 0) < lax.broadcasted_iota(jnp.int32, (t2, t2), 1)).astype(F32).astype(BF)
    expert_id = lax.broadcasted_iota(jnp.int32, (n_exp, t2), 0) + me * n_exp
    slot_id = lax.broadcasted_iota(jnp.int32, (slots, t2), 0).astype(F32)
    for q in range(4):
        iq = jnp.concatenate([idxall[2 * q], idxall[2 * q + 1]], axis=1)
        gq = jnp.concatenate([gateall[2 * q], gateall[2 * q + 1]], axis=1)
        hot = jnp.zeros((n_exp, t2), F32)
        gate = jnp.zeros((n_exp, t2), F32)
        for j in range(top_k):
            eq = iq[j:j + 1, :] == expert_id
            hot += jnp.where(eq, 1.0, 0.0)
            gate += jnp.where(eq, gq[j:j + 1, :], 0.0)
        pos = dot(hot.astype(BF), upper)
        code = jnp.where(hot > 0.5, pos, -1.0)
        gated = []
        for e in range(n_exp):
            eq = slot_id == code[e:e + 1, :]
            disp[q, e * slots:(e + 1) * slots, :] = jnp.where(eq, 1.0, 0.0).astype(BF)
            gated.append(jnp.where(eq, gate[e:e + 1, :], 0.0))
        comb[q] = jnp.concatenate(gated, axis=0).T.astype(BF)

    svc_a(1)
    svc_d(1)

    def gather_rows(k):
        for q in range(4):
            for hf in range(2):
                xq = xall[2 * k + hf, 2 * q:2 * q + 2].reshape(t2, KH)
                rows = dot(disp[q], xq).astype(BF)
                for e in range(n_exp):
                    xg[e, q * slots:(q + 1) * slots, hf * KH:(hf + 1) * KH] = rows[e * slots:(e + 1) * slots, :]

    def ex_groups(k, lo, hi):
        def group(g, carry):
            base = pre1 + k * n_exp + g * GRP

            def copy(i):
                n = base + i
                m = n - pre1
                src = w_in.at[m % n_exp, pl.ds((m // n_exp) * 2 * KH, 2 * KH), :]
                return pltpu.make_async_copy(src, ring1.at[n % NB1], g1.at[n % NB1])

            for i in range(GRP):
                copy(i).wait()
            for i in range(GRP):
                e = g * GRP + i
                z = dot(xg[e], ring1[(base + i) % NB1])
                if k > 0:
                    z += hacc[e]
                if k < nk - 1:
                    hacc[e] = z
                else:
                    hid[e] = gelu(z).astype(BF)

            @pl.when(base + NB1 < n_chunk1)
            def _():
                for i in range(GRP):
                    copy(i + NB1).start()
            return carry
        lax.fori_loop(lo, hi, group, 0)

    sh_out_half(0)
    sh_out_half(1)
    half_g = n_exp // GRP // 2
    svc_a(2)
    svc_d(2)
    for k in range(nk):
        partner_wait(2 * k)
        partner_wait(2 * k + 1)
        gather_rows(k)
        ex_groups(k, 0, half_g)
        svc_a(2 * k + 3)
        svc_d(2 * k + 3)
        ex_groups(k, half_g, 2 * half_g)
        svc_a(2 * k + 4)
        svc_d(2 * k + 4)

    def c0(b):
        return rcopy(pbuf.at[b % 2, 1 - core], r0.at[b % 4], p0s.at[b], p0r.at[b], pa)

    def c1(b, h):
        return rcopy(s1.at[b % 4, h], r1.at[b % 4, h], p1s.at[b, h], p1r.at[b, h], (xn, yn)[h])

    def c2(b, h):
        return rcopy(s2.at[b % 4, h], r2.at[b % 4, h], p2s.at[b, h], p2r.at[b, h], (yn, xn)[h])

    def svc1(b):
        c0(b).wait_recv()
        slot = b % 2
        rs = b % 4
        lo, hi = slice(0, CH), slice(CH, CB)

        def q_sum(q, cols):
            return pbuf[slot, core, q, :, cols] + r0[rs, q, :, cols]

        for i in range(2):
            s1[rs, 0, i] = q_sum(i * 2 + (1 - cx), lo)
            s1[rs, 1, i] = q_sum((1 - cy) * 2 + i, hi)
        c1(b, 0).start()
        c1(b, 1).start()
        s2[rs, 0] = q_sum(ychip, lo)
        s2[rs, 1] = q_sum(xchip, hi)
        acc[b, :, lo] += q_sum(chip, lo)
        acc[b, :, hi] += q_sum(chip, hi)
        c0(b).wait_send()

    def svc2(b):
        rs = b % 4
        c1(b, 0).wait_recv()
        c1(b, 1).wait_recv()
        s2[rs, 0] += r1[rs, 0, 1 - cy]
        c2(b, 0).start()
        s2[rs, 1] += r1[rs, 1, 1 - cx]
        c2(b, 1).start()
        acc[b, :, :CH] += r1[rs, 0, cy]
        acc[b, :, CH:] += r1[rs, 1, cx]

    def sends_done(b):
        for h in range(2):
            c1(b, h).wait_send()
            c2(b, h).wait_send()

    def fin(b):
        c2(b, 0).wait_recv()
        c2(b, 1).wait_recv()
        cols = pl.multiple_of(b * CB, CB)
        y_ref[:, pl.ds(cols, CH)] = (acc[b, :, :CH] + r2[b % 4, 0]).astype(BF)
        y_ref[:, pl.ds(pl.multiple_of(cols + CH, CH), CH)] = (acc[b, :, CH:] + r2[b % 4, 1]).astype(BF)

    def block(b, carry):
        for e in range(n_exp):
            copy2(b, e).wait()
        for e in range(n_exp):
            o = dot(hid[e], ring2[b % 2, e]).astype(BF)
            for q in range(4):
                obuf[q, e * slots:(e + 1) * slots, :] = o[q * slots:(q + 1) * slots, :]
        for q in range(4):
            part = dot(comb[q], obuf[q])
            pbuf[b % 2, 0, q] = part[:tok]
            pbuf[b % 2, 1, q] = part[tok:]
        c0(b).start()

        @pl.when(b + 2 < nb)
        def _():
            for e in range(n_exp):
                copy2(b + 2, e).start()

        @pl.when(b >= 5)
        def _():
            sends_done(b - 5)

        @pl.when(b >= 1)
        def _():
            svc1(b - 1)

        @pl.when(b >= 2)
        def _():
            svc2(b - 2)

        @pl.when(b >= 4)
        def _():
            fin(b - 4)
        return carry

    lax.fori_loop(0, nb, block, 0)
    sends_done(nb - 5)
    svc1(nb - 1)
    svc2(nb - 2)
    fin(nb - 4)
    svc2(nb - 1)
    for b in range(nb - 3, nb):
        fin(b)

    for cp in sent:
        cp.wait_send()
    for k in range(1, 8):
        for cp in meta_copies(k, me):
            cp.wait_send()
    for b in range(nb - 4, nb):
        sends_done(b)


def solution(mesh):
    group_size = mesh.shape['ep']

    def local_layer(x_loc, idx_loc, gate_loc, w_in, w_out, shared_in, shared_out):
        tok, top_k = idx_loc.shape
        n_exp, d_model, ff = w_in.shape
        n_sh = shared_in.shape[1] // ff
        cap = min(tok, LOAD_MULT * tok * top_k // (n_exp * group_size))
        slots = -(-2 * cap // 16) * 16
        rows = 4 * slots
        nh, nb = d_model // KH, d_model // CB
        any_spec = pl.BlockSpec(memory_space=pl.ANY)
        vmem_spec = pl.BlockSpec(memory_space=pltpu.VMEM)
        dma = pltpu.SemaphoreType.DMA
        return pl.pallas_call(
            functools.partial(kernel, top_k, slots),
            out_shape=jax.ShapeDtypeStruct((tok, d_model), BF),
            in_specs=[any_spec, vmem_spec, vmem_spec, any_spec, any_spec, any_spec, any_spec],
            out_specs=vmem_spec,
            scratch_shapes=[
                pltpu.VMEM((nh, group_size, tok, KH), BF),
                pltpu.VMEM((group_size, top_k, tok), jnp.int32),
                pltpu.VMEM((group_size, top_k, tok), F32),
                pltpu.VMEM((n_exp, rows, ff), F32),
                pltpu.VMEM((n_exp, rows, ff), BF),
                pltpu.VMEM((NB1, 2 * KH, ff), BF),
                pltpu.VMEM((2, n_exp, ff, CB), BF),
                pltpu.VMEM((n_exp, rows, 2 * KH), BF),
                pltpu.VMEM((4, n_exp * slots, 2 * tok), BF),
                pltpu.VMEM((4, 2 * tok, n_exp * slots), BF),
                pltpu.VMEM((4, n_exp * slots, CB), BF),
                pltpu.VMEM((2, 2, 4, tok, CB), F32),
                pltpu.VMEM((4, 4, tok, CB), F32),
                pltpu.VMEM((4, 2, 2, tok, CH), F32),
                pltpu.VMEM((4, 2, tok, CH), F32),
                pltpu.VMEM((4, 2, 2, tok, CH), F32),
                pltpu.VMEM((4, 2, tok, CH), F32),
                pltpu.VMEM((nb, tok, CB), F32),
                pltpu.VMEM((n_sh, tok, ff), BF),
                dma((nh, 7)), dma((nh, 8)), dma((7,)), dma((8,)), dma((7,)), dma((8,)), dma((nh,)), dma((NB1,)), dma((2, n_exp)),
                dma((nb,)), dma((nb,)), dma((nb, 2)), dma((nb, 2)), dma((nb, 2)), dma((nb, 2)),
            ],
            compiler_params=pltpu.CompilerParams(collective_id=0, has_side_effects=True, vmem_limit_bytes=67043328),
        )(x_loc, idx_loc.T, gate_loc.T, w_in, w_out, shared_in, shared_out)

    tok_spec = P(('dp', 'ep'), None)
    expert_spec = P('ep', None, None)
    whole_spec = P(None, None)
    return jax.shard_map(local_layer, mesh=mesh, in_specs=(tok_spec, tok_spec, tok_spec, expert_spec, expert_spec, whole_spec, whole_spec), out_specs=tok_spec, check_vma=False)
```

time: 104 us -> 91.1 us (0.88)
  Pallas kernels: 100 us -> 89 us
  other arithmetic: 2.04 us -> 0 us
    pallas_call x1, Pallas kernels: 100 us -> 89 us  [local_layer(): pl.pallas_call(functools.partial(kernel, top_k, slots), out_shape=jax.Sha...]
    concatenate x1 -> x0, other arithmetic: 1.36 us -> none  [local_layer(): jnp.concatenate([idx_loc.astype(F32).T, gate_loc.T, jnp.zeros((16 - 2 * t...]
where the time goes in v2:
time: 91.1 us; the launch traced here: 90.9 us
  Pallas kernels  89 us (98%)
  local copies, waits for them, and re-layouts  1.88 us (2%)
    pallas_call x1, Pallas kernels, local_layer(): pl.pallas_call(functools.partial(kernel, top_k, slots), out_shape=jax.Sha...  89 us
    unnamed x1, local copies, waits for them, and re-layouts  1.88 us

profile of v2, /device:TPU:0, one launch (start us, length us, event | category | flops | bytes accessed | tf_op | source)
XLA Modules:
  0.0 90.9 jit_solution(6483727127765030024)
XLA Ops:
  0.0 89.0 %shard_map.73 = bf16[128,2048]{1,0:T(8,128)(2,1)} custom-call(bf16[128,2048]{1,0:T(8,128)(2,1)} %x_hbm.1, s32[6,128]{1,0:T(8,128)} %bitcast.2, f32[6,128]{1,0:T(8,128)} %bitcast.3, bf16[8,2048,1408]{2,1,0:T(8,128)(2,1)} %w_in.1, bf16[8,1408,2048]{2,1,0:T(8,128)(2,1)} %w_out.1, bf16[2048,2816]{1,0:T(8,128)(2,1)} %sh_in.1, bf16[2816,2048]{1,0:T(8,128)(2,1)} %sh_out.1), custom_call_target="tpu_custom_call" | custom-call | tf_op jit(solution)/shard_map/pallas_call | solution.py:366
  89.0 1.9 %copy.9 = bf16[128,2048]{1,0:T(8,128)(2,1)} copy(bf16[128,2048]{1,0:T(8,128)(2,1)} %shard_map.73) | data formatting | bytes 1048576

commit v3 on v2

--- a/solution.py
+++ b/solution.py
@@ -12,6 +12,8 @@
 BF = jnp.bfloat16
 F32 = jnp.float32
 NB1 = 8
+MID = 6
+NB = 768
 GRP = 2
 KH = 256
 CB = 256
@@ -27,9 +29,9 @@
     return jnp.dot(a, b, preferred_element_type=F32)
 
 
-def kernel(top_k, slots, x_hbm, idx_ref, gate_ref, w_in, w_out, sh_in, sh_out, y_ref,
-           xall, idxall, gateall, hacc, hid, ring1, ring2, xg, disp, comb, obuf, pbuf, r0, r1, r2, s1, s2, acc, shid,
-           ag_s, ag_r, mi_s, mi_r, mg_s, mg_r, x_sem, g1, g2, p0s, p0r, p1s, p1r, p2s, p2r):
+def kernel(top_k, slots, x_hbm, idx_hbm, gate_hbm, w_in, w_out, sh_in, sh_out, y_hbm,
+           xall, idxall, gateall, hacc, hid, ring1, ring2, xg, disp, comb, obuf, pbuf, r0, r1, r2, s1, s2, acc, shid, ybuf,
+           ag_s, ag_r, mi_s, mi_r, mg_s, mg_r, m_sem, y_sem, x_sem, g1, g2, p0s, p0r, p1s, p1r, p2s, p2r):
     me = lax.axis_index('ep')
     n_exp, d_model, ff = w_in.shape
     tok = x_hbm.shape[0]
@@ -78,6 +80,10 @@
         return pltpu.make_async_copy(src, ring2.at[b % 2, e], g2.at[b % 2, e])
 
     xin = [pltpu.make_async_copy(x_hbm.at[:, pl.ds(j * KH, KH)], xall.at[j, me], x_sem.at[j]) for j in range(nh)]
+    routing = (pltpu.make_async_copy(idx_hbm, idxall.at[me], m_sem.at[0]),
+               pltpu.make_async_copy(gate_hbm, gateall.at[me], m_sem.at[1]))
+    for cp in routing:
+        cp.start()
     for cp in xin:
         cp.start()
     for i in range(NB1):
@@ -91,6 +97,8 @@
             copy2s(half, i).start()
     for cp in xin:
         cp.wait()
+    for cp in routing:
+        cp.wait()
     pl.semaphore_wait(barrier, 7)
 
     sent = []
@@ -129,14 +137,12 @@
 
     def meta_copies(k, o):
         dev = lax.rem(me + k, 8)
-        return (rcopy(idx_ref, idxall.at[o], mi_s.at[k - 1], mi_r.at[o], dev),
-                rcopy(gate_ref, gateall.at[o], mg_s.at[k - 1], mg_r.at[o], dev))
+        return (rcopy(idxall.at[o], idxall.at[o], mi_s.at[k - 1], mi_r.at[o], dev),
+                rcopy(gateall.at[o], gateall.at[o], mg_s.at[k - 1], mg_r.at[o], dev))
 
     for k in range(1, 8):
         for cp in meta_copies(k, me):
             cp.start()
-    idxall[me] = idx_ref[...]
-    gateall[me] = gate_ref[...]
     for j in range(1, nh):
         own(j)
 
@@ -213,13 +219,15 @@
                 copy(i).wait()
             for i in range(GRP):
                 e = g * GRP + i
-                z = dot(xg[e], ring1[(base + i) % NB1])
-                if k > 0:
-                    z += hacc[e]
-                if k < nk - 1:
-                    hacc[e] = z
-                else:
-                    hid[e] = gelu(z).astype(BF)
+                for col in range(0, ff, NB):
+                    ns = slice(col, min(col + NB, ff))
+                    z = dot(xg[e], ring1[(base + i) % NB1, :, ns])
+                    if k > 0:
+                        z += hacc[e, :, ns]
+                    if k < nk - 1:
+                        hacc[e, :, ns] = z
+                    else:
+                        hid[e, :, ns] = gelu(z).astype(BF)
 
             @pl.when(base + NB1 < n_chunk1)
             def _():
@@ -231,12 +239,13 @@
     sh_out_half(0)
     sh_out_half(1)
     half_g = n_exp // GRP // 2
-    svc_a(2)
-    svc_d(2)
     for k in range(nk):
         partner_wait(2 * k)
         partner_wait(2 * k + 1)
         gather_rows(k)
+        if k == 0:
+            svc_a(2)
+            svc_d(2)
         ex_groups(k, 0, half_g)
         svc_a(2 * k + 3)
         svc_d(2 * k + 3)
@@ -289,17 +298,29 @@
             c1(b, h).wait_send()
             c2(b, h).wait_send()
 
+    def out_copy(b):
+        return pltpu.make_async_copy(ybuf.at[b], y_hbm.at[:, pl.ds(pl.multiple_of(b * CB, CB), CB)], y_sem.at[b])
+
     def fin(b):
         c2(b, 0).wait_recv()
         c2(b, 1).wait_recv()
-        cols = pl.multiple_of(b * CB, CB)
-        y_ref[:, pl.ds(cols, CH)] = (acc[b, :, :CH] + r2[b % 4, 0]).astype(BF)
-        y_ref[:, pl.ds(pl.multiple_of(cols + CH, CH), CH)] = (acc[b, :, CH:] + r2[b % 4, 1]).astype(BF)
+        ybuf[b, :, :CH] = (acc[b, :, :CH] + r2[b % 4, 0]).astype(BF)
+        ybuf[b, :, CH:] = (acc[b, :, CH:] + r2[b % 4, 1]).astype(BF)
+        out_copy(b).start()
 
     def block(b, carry):
         for e in range(n_exp):
             copy2(b, e).wait()
         for e in range(n_exp):
+            if e == MID:
+                @pl.when(b >= 5)
+                def _():
+                    sends_done(b - 5)
+
+                @pl.when(b >= 1)
+                def _():
+                    svc1(b - 1)
+
             o = dot(hid[e], ring2[b % 2, e]).astype(BF)
             for q in range(4):
                 obuf[q, e * slots:(e + 1) * slots, :] = o[q * slots:(q + 1) * slots, :]
@@ -314,14 +335,6 @@
             for e in range(n_exp):
                 copy2(b + 2, e).start()
 
-        @pl.when(b >= 5)
-        def _():
-            sends_done(b - 5)
-
-        @pl.when(b >= 1)
-        def _():
-            svc1(b - 1)
-
         @pl.when(b >= 2)
         def _():
             svc2(b - 2)
@@ -347,6 +360,8 @@
             cp.wait_send()
     for b in range(nb - 4, nb):
         sends_done(b)
+    for b in range(nb):
+        out_copy(b).wait()
 
 
 def solution(mesh):
@@ -361,13 +376,12 @@
         rows = 4 * slots
         nh, nb = d_model // KH, d_model // CB
         any_spec = pl.BlockSpec(memory_space=pl.ANY)
-        vmem_spec = pl.BlockSpec(memory_space=pltpu.VMEM)
         dma = pltpu.SemaphoreType.DMA
         return pl.pallas_call(
             functools.partial(kernel, top_k, slots),
             out_shape=jax.ShapeDtypeStruct((tok, d_model), BF),
-            in_specs=[any_spec, vmem_spec, vmem_spec, any_spec, any_spec, any_spec, any_spec],
-            out_specs=vmem_spec,
+            in_specs=[any_spec, any_spec, any_spec, any_spec, any_spec, any_spec, any_spec],
+            out_specs=any_spec,
             scratch_shapes=[
                 pltpu.VMEM((nh, group_size, tok, KH), BF),
                 pltpu.VMEM((group_size, top_k, tok), jnp.int32),
@@ -388,7 +402,8 @@
                 pltpu.VMEM((4, 2, tok, CH), F32),
                 pltpu.VMEM((nb, tok, CB), F32),
                 pltpu.VMEM((n_sh, tok, ff), BF),
-                dma((nh, 7)), dma((nh, 8)), dma((7,)), dma((8,)), dma((7,)), dma((8,)), dma((nh,)), dma((NB1,)), dma((2, n_exp)),
+                pltpu.VMEM((nb, tok, CB), BF),
+                dma((nh, 7)), dma((nh, 8)), dma((7,)), dma((8,)), dma((7,)), dma((8,)), dma((2,)), dma((nb,)), dma((nh,)), dma((NB1,)), dma((2, n_exp)),
                 dma((nb,)), dma((nb,)), dma((nb, 2)), dma((nb, 2)), dma((nb, 2)), dma((nb, 2)),
             ],
             compiler_params=pltpu.CompilerParams(collective_id=0, has_side_effects=True, vmem_limit_bytes=67043328),

time: 91.1 us -> 89.1 us (0.978)
  Pallas kernels: 89 us -> 87 us
    pallas_call x1, Pallas kernels: 89 us -> 87 us  [local_layer(): pl.pallas_call(functools.partial(kernel, top_k, slots), out_shape=jax.Sha...]
where the time goes in v3:
time: 89.1 us; the launch traced here: 88.9 us
  Pallas kernels  87 us (98%)
  local copies, waits for them, and re-layouts  1.88 us (2%)
    pallas_call x1, Pallas kernels, local_layer(): pl.pallas_call(functools.partial(kernel, top_k, slots), out_shape=jax.Sha...  87 us
    unnamed x1, local copies, waits for them, and re-layouts  1.88 us

profile of v3, /device:TPU:0, one launch (start us, length us, event | category | flops | bytes accessed | tf_op | source)
XLA Modules:
  0.0 88.9 jit_solution(11574742847801701358)
XLA Ops:
  0.0 87.0 %shard_map.73 = bf16[128,2048]{1,0:T(8,128)(2,1)} custom-call(bf16[128,2048]{1,0:T(8,128)(2,1)} %x_hbm.1, s32[6,128]{1,0:T(8,128)} %bitcast.2, f32[6,128]{1,0:T(8,128)} %bitcast.3, bf16[8,2048,1408]{2,1,0:T(8,128)(2,1)} %w_in.1, bf16[8,1408,2048]{2,1,0:T(8,128)(2,1)} %w_out.1, bf16[2048,2816]{1,0:T(8,128)(2,1)} %sh_in.1, bf16[2816,2048]{1,0:T(8,128)(2,1)} %sh_out.1), custom_call_target="tpu_custom_call" | custom-call | tf_op jit(solution)/shard_map/pallas_call | solution.py:380
  87.1 1.9 %copy.9 = bf16[128,2048]{1,0:T(8,128)(2,1)} copy(bf16[128,2048]{1,0:T(8,128)(2,1)} %shard_map.73) | data formatting | bytes 1048576
